TPU v7x, 128 devices: a whole 4x4x4 slice. The times are simulated.
128 devices in a mesh: rep: 4 (over z_hi, core), row: 4 (over x), col: 8 (over z_lo, y).
Axes of the slice: x: 4, y: 4, z: 4 (z_hi: 2, z_lo: 2; z = z_hi * 2 + z_lo), core: 2. Of those that a mesh axis runs over, the one named last changes fastest.
Arguments:
- grad_parts: bfloat16 [4, 16384, 6144], P('rep', ('row', 'col')), may hold values from -0.03125 to 0.03125, as said below
- statistic: float32 [6144, 6144], P('row', 'col'), may hold values from -150 to 150, as said below
Outputs:
- gram_matrix: float32 [6144, 6144], P('row', 'col')
- statistic_next: float32 [6144, 6144], P('row', 'col')
Inputs may be any that keep to these rules, and one draw needn't show every extreme that they name: Every entry of grad_parts has a magnitude between 2^-10 and 2^-5. statistic is symmetric and positive definite.
All inputs are finite; a program needn't handle non-finite values.
Results may differ from a plain program's by a relative error of at most 0.008.
Values may be sent and summed in bfloat16 or wider, within the bound.
A program may use at most 128 MiB of HBM per device.

v0:
```python
import jax
import jax.numpy as jnp
from jax import lax
from jax.sharding import PartitionSpec as P


def shards(grad_parts, statistic):
    own_part = grad_parts[0].astype(jnp.float32)
    summed = lax.psum_scatter(own_part.astype(jnp.bfloat16), "rep", scatter_dimension=0, tiled=True)
    rows_panel = lax.all_to_all(summed, "row", split_axis=1, concat_axis=0, tiled=True)
    cols_panel = lax.all_to_all(summed, "col", split_axis=1, concat_axis=0, tiled=True)
    row_count = lax.axis_size("row")
    col_count = lax.axis_size("col")
    quarter = summed.shape[0]
    right_whole = lax.all_gather(cols_panel, "row", axis=0, tiled=True)
    right_order = (
        right_whole.reshape(row_count, col_count, quarter, -1)
        .transpose(1, 0, 2, 3)
        .reshape(row_count * col_count * quarter, -1)
    )
    partial_tile = lax.dot_general(
        lax.all_gather(rows_panel, "col", axis=0, tiled=True),
        right_order,
        (((0,), (0,)), ((), ())),
        preferred_element_type=jnp.float32,
    )
    portion = lax.psum_scatter(partial_tile, "rep", scatter_dimension=0, tiled=True)
    gram_tile = lax.all_gather(portion, "rep", axis=0, tiled=True)
    return (gram_tile, 0.95 * statistic + 0.05 * gram_tile)


def solution(mesh):
    return jax.shard_map(
        shards,
        mesh=mesh,
        in_specs=(P("rep", ("row", "col"), None), P("row", "col")),
        out_specs=(P("row", "col"), P("row", "col")),
        check_vma=False,
    )
```

profile of v0, /device:TPU:1, one launch (start us, length us, event | category | flops | bytes accessed | tf_op | source)
XLA Modules:
  0.0 441.3 jit_solution(476243138658292207)
XLA Ops:
  7.2 0.0 reduce-scatter.7.cloned.1.call-start
  7.2 0.7 reduce-scatter.7.cloned.1.call-update
  7.9 0.0 all-gather.6.cloned.1.call-start
  7.9 71.7 %reduce-scatter.7.cloned.1.call-done = bf16[128,6144]{1,0:T(8,128)(2,1)} async-done(((bf16[512,6144]{1,0:T(8,128)(2,1)}), bf16[128,6144]{1,0:T(8,128)(2,1)}) %reduce-scatter.7.cloned.1.call-update) | async-done | bytes 1572880
  79.6 1.9 copy.14
  81.5 24.2 %all_to_all.38 = bf16[128,8,768]{0,2,1:T(8,128)(2,1)S(1)} all-to-all(bf16[128,8,768]{0,2,1:T(8,128)(2,1)S(1)} %bitcast.15), channel_id=1, replica_groups=mesh['rep'=4,'row'=4,'col'=8] {'col'}, dimensions={1} | all-to-all | bytes 3145728 | tf_op jit(solution)/shard_map/all_to_all | solution.py:11
  105.7 1.6 copy.11
  107.3 0.0 all-gather.6.cloned.1.call-update
  107.3 0.0 all-gather.4.cloned.1.call-start
  107.3 29.4 %all_to_all.39 = bf16[128,4,1536]{0,2,1:T(8,128)(2,1)S(1)} all-to-all(bf16[128,4,1536]{0,2,1:T(8,128)(2,1)S(1)} %bitcast.16), channel_id=1, replica_groups=mesh['rep'=4,'row'=4,'col'=8] {'row'}, dimensions={1} | all-to-all | bytes 3145728 | tf_op jit(solution)/shard_map/all_to_all | solution.py:10
  136.7 1.6 copy.10
  138.3 0.0 all-gather.4.cloned.1.call-update
  138.3 0.0 reduce-scatter.5.cloned.1.call-start
  138.4 44.5 %all-gather.6.cloned.1.call-done = bf16[4096,768]{1,0:T(8,128)(2,1)} async-done(((bf16[1024,768]{1,0:T(8,128)(2,1)}), bf16[4096,768]{1,0:T(8,128)(2,1)}) %all-gather.6.cloned.1.call-update) | async-done | bytes 6291472 | tf_op jit(solution)/shard_map/all_gather | solution.py:15
  182.9 6.0 %copy.12 = bf16[4,8,128,768]{3,2,0,1:T(8,128)(2,1)} copy(bf16[4,8,128,768]{3,2,1,0:T(8,128)(2,1)} %bitcast.18) | data formatting | bytes 12582912 | tf_op jit(solution)/shard_map/reshape | solution.py:17
  188.9 123.7 %all-gather.4.cloned.1.call-done = bf16[4096,1536]{1,0:T(8,128)(2,1)} async-done(((bf16[512,1536]{1,0:T(8,128)(2,1)}), bf16[4096,1536]{1,0:T(8,128)(2,1)}) %all-gather.4.cloned.1.call-update) | async-done | bytes 12582928 | tf_op jit(solution)/shard_map/all_gather | solution.py:22
  312.6 16.4 %fusion = f32[1536,768]{1,0:T(8,128)} fusion(bf16[4096,1536]{1,0:T(8,128)(2,1)} %all-gather.4.cloned.1.call-done, bf16[4096,768]{1,0:T(8,128)(2,1)} %bitcast.19), kind=kOutput, calls=%fused_computation.1 | convolution fusion | flops 9663676416 | bytes 23592960 | tf_op jit(solution)/shard_map/dot_general | solution.py:21
  328.9 0.0 reduce-scatter.5.cloned.1.call-update
  328.9 0.0 all-gather.8.cloned.1.call-start
  329.0 53.8 %reduce-scatter.5.cloned.1.call-done = f32[384,768]{1,0:T(8,128)} async-done(((f32[1536,768]{1,0:T(8,128)}), f32[384,768]{1,0:T(8,128)}) %reduce-scatter.5.cloned.1.call-update) | async-done | bytes 1179664 | tf_op jit(solution)/shard_map/reduce_scatter | solution.py:27
  382.8 0.0 all-gather.8.cloned.1.call-update
  382.8 42.9 %all-gather.8.cloned.1.call-done = f32[1536,768]{1,0:T(8,128)} async-done(((f32[384,768]{1,0:T(8,128)}), f32[1536,768]{1,0:T(8,128)}) %all-gather.8.cloned.1.call-update) | async-done | bytes 4718608 | tf_op jit(solution)/shard_map/all_gather | solution.py:28
  425.7 0.0 copy-start
  425.7 6.8 %multiply_add_fusion = f32[1536,768]{1,0:T(8,128)} fusion(f32[1536,768]{1,0:T(8,128)} %all-gather.8.cloned.1.call-done, f32[1536,768]{1,0:T(8,128)} %param.3), kind=kLoop, calls=%fused_computation | loop fusion | flops 3538944 | bytes 14155776 | tf_op jit(solution)/shard_map/add | solution.py:29
  432.6 0.0 copy-done
  432.6 2.2 copy.17
Async XLA Ops:
  7.2 72.4 %reduce-scatter.7.cloned.1.call-start = ((), (), s32[]{:S(2)}) async-start(), calls=%async_computation.8 | async-start | bytes 7864320
  7.9 175.0 %all-gather.6.cloned.1.call-start = ((), (), s32[]{:S(2)}) async-start(), calls=%async_computation.5 | async-start | bytes 7864320 | tf_op jit(solution)/shard_map/all_gather | solution.py:15
  107.3 205.3 %all-gather.4.cloned.1.call-start = ((), (), s32[]{:S(2)}) async-start(), calls=%async_computation.4 | async-start | bytes 14155776 | tf_op jit(solution)/shard_map/all_gather | solution.py:22
  138.3 244.5 %reduce-scatter.5.cloned.1.call-start = ((), (), s32[]{:S(2)}) async-start(), calls=%async_computation.6 | async-start | bytes 5898240 | tf_op jit(solution)/shard_map/reduce_scatter | solution.py:27
  328.9 96.8 %all-gather.8.cloned.1.call-start = ((), (), s32[]{:S(2)}) async-start(), calls=%async_computation.7 | async-start | bytes 5898240 | tf_op jit(solution)/shard_map/all_gather | solution.py:28
  425.7 6.9 %copy-start = (f32[1536,768]{1,0:T(8,128)S(1)}, f32[1536,768]{1,0:T(8,128)}, u32[]{:S(2)}) copy-start(f32[1536,768]{1,0:T(8,128)} %all-gather.8.cloned.1.call-done) | copy-start | bytes 14155780
Sparse Core Ops, SparseCore 0:
  10.6 68.9 reduce-scatter.6
  107.4 75.4 all-gather.5
  185.1 127.4 all-gather.3
  329.1 53.6 reduce-scatter.4
  384.3 41.3 all-gather.7
where the time goes:
time: 442 us; the launch traced here: 441 us
  waiting for transfers between devices  337 us (76%)
  blocking collectives  53.6 us (12%)
  matrix products  16.4 us (4%)
  between operations  13.8 us (3%)
  local copies, waits for them, and re-layouts  13.3 us (3%)
  other arithmetic  6.85 us (2%)
    all_gather x1, waiting for transfers between devices, shards(): lax.all_gather(rows_panel, 'col', axis=0, tiled=True)  124 us
    unnamed x6, waiting for transfers between devices  72.4 us
    reduce_scatter x1, waiting for transfers between devices, shards(): lax.psum_scatter(partial_tile, 'rep', scatter_dimension=0, tiled=True)  53.8 us
    all_gather x1, waiting for transfers between devices, shards(): right_whole = lax.all_gather(cols_panel, 'row', axis=0, tiled=True)  44.5 us
    all_gather x1, waiting for transfers between devices, shards(): gram_tile = lax.all_gather(portion, 'rep', axis=0, tiled=True)  42.9 us
    all_to_all x1, blocking collectives, shards(): lax.all_to_all(summed, 'row', split_axis=1, concat_axis=0, tiled=True)  29.4 us
    all_to_all x1, blocking collectives, shards(): lax.all_to_all(summed, 'col', split_axis=1, concat_axis=0, tiled=True)  24.2 us
    dot_general x1, matrix products, shards(): lax.dot_general(lax.all_gather(rows_panel, 'col', axis=0, tiled=True), ri...  16.4 us
  transfers between devices with their start and end apart: 5, of which 5 were waited for; matrix products, arithmetic and copies ran while one was open for 2% of the time, Pallas kernels for 0%

commit v1 on v0

--- a/solution.py
+++ b/solution.py
@@ -12,7 +12,12 @@
     row_count = lax.axis_size("row")
     col_count = lax.axis_size("col")
     quarter = summed.shape[0]
-    right_whole = lax.all_gather(cols_panel, "row", axis=0, tiled=True)
+    ring = [cols_panel]
+    for hop in range(3):
+        ring.append(lax.ppermute(ring[-1], "row", [(dev, (dev + 1) % 4) for dev in range(4)]))
+    right_whole = jnp.roll(
+        jnp.concatenate(ring[::-1], axis=0), (lax.axis_index("row") + 1) * ring[0].shape[0], axis=0
+    )
     right_order = (
         right_whole.reshape(row_count, col_count, quarter, -1)
         .transpose(1, 0, 2, 3)

time: 442 us -> 404 us (0.914)
  waiting for transfers between devices: 337 us -> 266 us
  local copies, waits for them, and re-layouts: 13.3 us -> 44.3 us
    all_gather x1, waiting for transfers between devices: 124 us -> 0.01 us  [shards(): lax.all_gather(rows_panel, 'col', axis=0, tiled=True)]
    ppermute x0 -> x3, waiting for transfers between devices: none -> 93.6 us  [shards(): lax.ppermute(ring[-1], 'row', [(dev, (dev + 1) % 4) for dev in range(4)])]
    all_gather x1 -> x0, waiting for transfers between devices: 44.5 us -> none  [shards(): right_whole = lax.all_gather(cols_panel, 'row', axis=0, tiled=True)]
    unnamed x4 -> x11, local copies, waits for them, and re-layouts: 4.1 us -> 34.5 us
    reduce_scatter x1, waiting for transfers between devices: 53.8 us -> 63.7 us  [shards(): lax.psum_scatter(partial_tile, 'rep', scatter_dimension=0, tiled=True)]
    all_to_all x1, blocking collectives: 24.2 us -> 31.5 us  [shards(): lax.all_to_all(summed, 'col', split_axis=1, concat_axis=0, tiled=True)]
    all_gather x1, waiting for transfers between devices: 42.9 us -> 36.9 us  [shards(): gram_tile = lax.all_gather(portion, 'rep', axis=0, tiled=True)]
    reshape x1 -> x0, local copies, waits for them, and re-layouts: 6.04 us -> none  [shards(): right_whole.reshape(row_count, col_count, quarter, -1).transpose(1, 0, 2, 3)]
  transfers between devices with their start and end apart: 5 -> 7, of which waited for: 5 -> 6; matrix products, arithmetic and copies ran while one was open for 2% -> 7% of each run, Pallas kernels for 0% -> 0%
where the time goes in v1:
time: 404 us; the launch traced here: 403 us
  waiting for transfers between devices  266 us (66%)
  blocking collectives  55 us (14%)
  local copies, waits for them, and re-layouts  44.3 us (11%)
  matrix products  16.3 us (4%)
  between operations  13.8 us (3%)
  other arithmetic  7.07 us (2%)
    ppermute x3, waiting for transfers between devices, shards(): lax.ppermute(ring[-1], 'row', [(dev, (dev + 1) % 4) for dev in range(4)])  93.6 us
    unnamed x5, waiting for transfers between devices  72.4 us
    reduce_scatter x1, waiting for transfers between devices, shards(): lax.psum_scatter(partial_tile, 'rep', scatter_dimension=0, tiled=True)  63.7 us
    all_gather x1, waiting for transfers between devices, shards(): gram_tile = lax.all_gather(portion, 'rep', axis=0, tiled=True)  36.9 us
    unnamed x11, local copies, waits for them, and re-layouts  34.5 us
    all_to_all x1, blocking collectives, shards(): lax.all_to_all(summed, 'col', split_axis=1, concat_axis=0, tiled=True)  31.5 us
    all_to_all x1, blocking collectives, shards(): lax.all_to_all(summed, 'row', split_axis=1, concat_axis=0, tiled=True)  23.5 us
    dot_general x1, matrix products, shards(): lax.dot_general(lax.all_gather(rows_panel, 'col', axis=0, tiled=True), ri...  16.3 us
  transfers between devices with their start and end apart: 7, of which 6 were waited for; matrix products, arithmetic and copies ran while one was open for 7% of the time, Pallas kernels for 0%

profile of v1, /device:TPU:1, one launch (start us, length us, event | category | flops | bytes accessed | tf_op | source)
XLA Modules:
  0.0 403.1 jit_solution(6673578233469608987)
XLA Ops:
  7.2 0.0 reduce-scatter.7.cloned.1.call-start
  7.2 0.7 reduce-scatter.7.cloned.1.call-update
  7.9 0.0 all-gather.3.cloned.1.call-start
  7.9 71.7 %reduce-scatter.7.cloned.1.call-done = bf16[128,6144]{1,0:T(8,128)(2,1)} async-done(((bf16[512,6144]{1,0:T(8,128)(2,1)}), bf16[128,6144]{1,0:T(8,128)(2,1)}) %reduce-scatter.7.cloned.1.call-update) | async-done | bytes 1572880
  79.6 1.9 copy.25
  81.5 23.5 %all_to_all.38 = bf16[128,4,1536]{0,2,1:T(8,128)(2,1)S(1)} all-to-all(bf16[128,4,1536]{0,2,1:T(8,128)(2,1)S(1)} %bitcast.21), channel_id=1, replica_groups=mesh['rep'=4,'row'=4,'col'=8] {'row'}, dimensions={1} | all-to-all | bytes 3145728 | tf_op jit(solution)/shard_map/all_to_all | solution.py:10
  105.0 1.6 copy.20
  106.5 0.0 reduce-scatter.5.cloned.1.call-start
  106.6 31.5 %all_to_all.39 = bf16[128,8,768]{0,2,1:T(8,128)(2,1)S(1)} all-to-all(bf16[128,8,768]{0,2,1:T(8,128)(2,1)S(1)} %bitcast.22), channel_id=1, replica_groups=mesh['rep'=4,'row'=4,'col'=8] {'col'}, dimensions={1} | all-to-all | bytes 3145728 | tf_op jit(solution)/shard_map/all_to_all | solution.py:11
  138.1 0.7 copy.18
  138.8 0.1 collective-permute-start
  138.9 27.7 %collective-permute-done = bf16[1024,768]{1,0:T(8,128)(2,1)S(1)} collective-permute-done((bf16[1024,768]{1,0:T(8,128)(2,1)S(1)}, bf16[1024,768]{1,0:T(8,128)(2,1)S(1)}, u32[]{:S(2)}, u32[]{:S(2)}) %collective-permute-start) | collective-permute-done | bytes 1572896 | tf_op jit(solution)/shard_map/ppermute | solution.py:17
  166.6 33.0 %collective-permute-done.1 = bf16[1024,768]{1,0:T(8,128)(2,1)} collective-permute-done((bf16[1024,768]{1,0:T(8,128)(2,1)S(1)}, bf16[1024,768]{1,0:T(8,128)(2,1)}, u32[]{:S(2)}, u32[]{:S(2)}) %collective-permute-start.1) | collective-permute-done | bytes 1572896 | tf_op jit(solution)/shard_map/ppermute | solution.py:17
  199.6 32.9 %collective-permute-done.2 = bf16[1024,768]{1,0:T(8,128)(2,1)} collective-permute-done((bf16[1024,768]{1,0:T(8,128)(2,1)}, bf16[1024,768]{1,0:T(8,128)(2,1)}, u32[]{:S(2)}, u32[]{:S(2)}) %collective-permute-start.2) | collective-permute-done | bytes 1572896 | tf_op jit(solution)/shard_map/ppermute | solution.py:17
  232.5 2.7 constant_dynamic-update-slice_fusion.7
  235.1 2.7 constant_dynamic-update-slice_fusion.6
  237.8 1.2 constant_dynamic-update-slice_fusion.5
  239.1 1.3 constant_dynamic-update-slice_fusion.4
  240.3 2.7 constant_dynamic-update-slice_fusion.3
  243.0 2.6 constant_dynamic-update-slice_fusion.2
  245.7 1.3 constant_dynamic-update-slice_fusion.1
  247.0 1.3 constant_dynamic-update-slice_fusion
  248.2 3.2 constant_dynamic-slice_fusion
  251.4 3.0 copy.19
  254.4 16.3 %convolution_bitcast_fusion = f32[1536,768]{0,1:T(8,128)} fusion(bf16[4096,768]{1,0:T(8,128)(2,1)} %bitcast.24, bf16[4096,1536]{1,0:T(8,128)(2,1)} %all-gather.3.cloned.1.call-done), kind=kOutput, calls=%fused_computation.1 | convolution fusion | flops 9663676416 | bytes 23592960 | tf_op jit(solution)/shard_map/dot_general | solution.py:26
  270.8 0.0 all-gather.5.cloned.1.call-start
  270.8 63.7 %reduce-scatter.5.cloned.1.call-done = f32[384,768]{0,1:T(8,128)} async-done(((f32[1536,768]{0,1:T(8,128)}), f32[384,768]{0,1:T(8,128)}) %reduce-scatter.5.cloned.1.call-update) | async-done | bytes 1179664 | tf_op jit(solution)/shard_map/reduce_scatter | solution.py:32
  334.5 6.0 %copy.21 = f32[1536,768]{0,1:T(8,128)} copy(f32[1536,768]{1,0:T(8,128)} %param.3) | data formatting | bytes 9437184 | tf_op args[1]
  340.6 36.9 %all-gather.5.cloned.1.call-done = f32[1536,768]{0,1:T(8,128)} async-done(((f32[384,768]{0,1:T(8,128)}), f32[1536,768]{0,1:T(8,128)}) %all-gather.5.cloned.1.call-update) | async-done | bytes 4718608 | tf_op jit(solution)/shard_map/all_gather | solution.py:33
  377.4 7.1 %multiply_add_fusion = f32[1536,768]{0,1:T(8,128)} fusion(f32[1536,768]{0,1:T(8,128)} %all-gather.5.cloned.1.call-done, f32[1536,768]{0,1:T(8,128)} %copy.21), kind=kLoop, calls=%fused_computation | loop fusion | flops 3538944 | bytes 14155776 | tf_op jit(solution)/shard_map/add | solution.py:34
  384.5 6.0 %copy.23 = f32[1536,768]{1,0:T(8,128)} copy(f32[1536,768]{0,1:T(8,128)} %multiply_add_fusion) | data formatting | bytes 9437184
  390.5 6.0 %copy.22 = f32[1536,768]{1,0:T(8,128)} copy(f32[1536,768]{0,1:T(8,128)} %all-gather.5.cloned.1.call-done) | data formatting | bytes 9437184
  (6 shorter events, 0.1 us)
Async XLA Ops:
  7.2 72.4 %reduce-scatter.7.cloned.1.call-start = ((), (), s32[]{:S(2)}) async-start(), calls=%async_computation.7 | async-start | bytes 7864320
  7.9 246.5 %all-gather.3.cloned.1.call-start = ((), (), s32[]{:S(2)}) async-start(), calls=%async_computation.4 | async-start | bytes 14155776 | tf_op jit(solution)/shard_map/all_gather | solution.py:27
  106.5 227.9 %reduce-scatter.5.cloned.1.call-start = ((), (), s32[]{:S(2)}) async-start(), calls=%async_computation.5 | async-start | bytes 5898240 | tf_op jit(solution)/shard_map/reduce_scatter | solution.py:32
  138.8 27.8 %collective-permute-start = (bf16[1024,768]{1,0:T(8,128)(2,1)S(1)}, bf16[1024,768]{1,0:T(8,128)(2,1)S(1)}, u32[]{:S(2)}, u32[]{:S(2)}) collective-permute-start(bf16[1024,768]{1,0:T(8,128)(2,1)S(1)} %bitcast.18), channel_id=1, source_target_pairs={{0,8},{8,16},{16,24},{24,0},{1,9},{9,17},{17,25},{25,1},{2,10},{10... | collective-permute-start | bytes 4718600 | tf_op jit(solution)/shard_map/ppermute | solution.py:17
  166.6 33.0 %collective-permute-start.1 = (bf16[1024,768]{1,0:T(8,128)(2,1)S(1)}, bf16[1024,768]{1,0:T(8,128)(2,1)}, u32[]{:S(2)}, u32[]{:S(2)}) collective-permute-start(bf16[1024,768]{1,0:T(8,128)(2,1)S(1)} %collective-permute-done), channel_id=1, source_target_pairs={{0,8},{8,16},{16,24},{24,0},{1,9},{9,17},{17,25},{25,1},{2,10},{10... | collective-permute-start | bytes 4718600 | tf_op jit(solution)/shard_map/ppermute | solution.py:17
  199.6 32.9 %collective-permute-start.2 = (bf16[1024,768]{1,0:T(8,128)(2,1)}, bf16[1024,768]{1,0:T(8,128)(2,1)}, u32[]{:S(2)}, u32[]{:S(2)}) collective-permute-start(bf16[1024,768]{1,0:T(8,128)(2,1)} %collective-permute-done.1), channel_id=1, source_target_pairs={{0,8},{8,16},{16,24},{24,0},{1,9},{9,17},{17,25},{25,1},{2,10},{10... | collective-permute-start | bytes 4718600 | tf_op jit(solution)/shard_map/ppermute | solution.py:17
  270.8 106.7 %all-gather.5.cloned.1.call-start = ((), (), s32[]{:S(2)}) async-start(), calls=%async_computation.6 | async-start | bytes 5898240 | tf_op jit(solution)/shard_map/all_gather | solution.py:33
Sparse Core Ops, SparseCore 0:
  10.6 68.9 reduce-scatter.6
  106.7 144.1 all-gather.2
  270.9 63.5 reduce-scatter.4
  336.0 41.3 all-gather.4
